TPU v7x, 32 devices: a whole 2x2x4 slice. The times are simulated.
32 devices in a mesh: grp: 8 (over z, y), lane: 4 (over x, core).
Axes of the slice: x: 2, y: 2, z: 4, core: 2. Of those that a mesh axis runs over, the one named last changes fastest.
Arguments:
- grad_pooled: bfloat16 [4096, 16, 256], P(('grp', 'lane')), may hold values from -16 to 16
- bag_len: int32 [4096, 16], P(('grp', 'lane')), may hold values from 1 to 8
- lookup_slot: int32 [4096, 16, 8], P('grp', 'lane'), may hold values from -1 to 15, as said below
- slot_row: int32 [8, 4, 8, 2], P('grp', 'lane'), may hold values from 0 to 1023, as said below
- weights: float32 [16, 2048, 256], P('lane', 'grp'), may hold values from -6 to 6
- accum: float32 [16, 2048], P('lane', 'grp'), may hold values from 0.05 to 0.5
Outputs:
- new_weights: float32 [16, 2048, 256], P('lane', 'grp')
- new_accum: float32 [16, 2048], P('lane', 'grp')
Inputs may be any that keep to these rules, and one draw needn't show every extreme that they name: `lookup_slot`: position j of bag (b, t) holds -1 when j >= bag_len[b, t] and otherwise a slot number s; the row slot_row[s // 2, t // 4, g, s % 2], with g the group of sample b, lies in local table t % 4. `slot_row`: several slots, also from different groups, may name the same row.
All inputs are finite; a program needn't handle non-finite values.
Results may differ from a plain program's by a relative error of at most 0.0035.
Values may be sent and summed in bfloat16 or wider, within the bound.
A program may use at most 64 MiB of HBM per device.

v0:
```python
import math
import jax
import jax.numpy as jnp
from jax import lax
from jax.sharding import PartitionSpec as P

SLOTS_PEER = 2
LEARN_RATE = 0.3
EPSILON = 1e-06


def per_device(grad_pooled, bag_len, lookup_slot, slot_row, weights, accum):
    lane_count = lax.axis_size("lane")
    group_count = lax.axis_size("grp")
    number_slots = group_count * SLOTS_PEER
    batch_rows, table_count, embed_width = grad_pooled.shape
    tables_here = table_count // lane_count
    bag_depth = lookup_slot.shape[2]
    scaled = (grad_pooled.astype(jnp.float32) / bag_len.astype(jnp.float32)[:, :, None]).astype(
        jnp.bfloat16
    )
    own_slots = lax.all_to_all(lookup_slot, "lane", split_axis=0, concat_axis=1, tiled=True)
    slot_marks = jnp.transpose(
        own_slots.reshape(batch_rows, lane_count, tables_here, bag_depth), (1, 0, 2, 3)
    )
    numbers = lax.broadcasted_iota(jnp.int32, (1, number_slots, 1, 1, 1), 1)
    counts = jnp.sum(slot_marks[:, None] == numbers, axis=-1, dtype=jnp.int32).astype(jnp.bfloat16)
    values = scaled.reshape(batch_rows, lane_count, tables_here, embed_width)
    partial_here = jnp.einsum(
        "msbt,bmte->mse", counts, values, preferred_element_type=jnp.float32
    ).astype(jnp.bfloat16)
    partial_value = lax.all_to_all(partial_here, "lane", split_axis=0, concat_axis=0, tiled=True)
    slot_sum = jnp.sum(partial_value.astype(jnp.float32), axis=0).astype(jnp.bfloat16)
    outgoing = slot_sum.reshape(group_count, SLOTS_PEER, embed_width)
    incoming = lax.all_to_all(outgoing, "grp", split_axis=0, concat_axis=0, tiled=True).reshape(
        number_slots, embed_width
    )
    targets = slot_row.reshape(1, number_slots)
    local_rows = accum.shape[0] * accum.shape[1]
    row_ids = lax.broadcasted_iota(jnp.int32, (local_rows, 1), 0)
    placing = (row_ids == targets).astype(jnp.bfloat16)
    row_grad = jnp.dot(placing, incoming, preferred_element_type=jnp.float32)
    square_mean = jnp.mean(row_grad * row_grad, axis=1)
    norm_total = lax.psum(embed_width * jnp.sum(square_mean), ("grp", "lane"))
    clip_limit = 0.5 * math.sqrt(group_count * lane_count * number_slots * embed_width)
    clip_factor = clip_limit / jnp.maximum(jnp.sqrt(norm_total), clip_limit)
    new_accum = accum + clip_factor * clip_factor * square_mean.reshape(accum.shape)
    step_rows = LEARN_RATE * clip_factor * row_grad.reshape(weights.shape)
    new_weights = weights - step_rows / (jnp.sqrt(new_accum)[:, :, None] + EPSILON)
    return (new_weights, new_accum)


def solution(mesh):
    placed = (
        P(("grp", "lane"), None, None),
        P(("grp", "lane"), None),
        P("grp", "lane", None),
        P("grp", "lane", None, None),
        P("lane", "grp", None),
        P("lane", "grp"),
    )
    return jax.shard_map(
        per_device,
        mesh=mesh,
        in_specs=placed,
        out_specs=(P("lane", "grp", None), P("lane", "grp")),
        check_vma=False,
    )
```

profile of v0, /device:TPU:0, one launch (start us, length us, event | category | flops | bytes accessed | tf_op | source)
XLA Modules:
  0.0 79.0 jit_solution(7309163360748396572)
XLA Ops:
  0.6 1.3 %copy.21 = s32[512,4,8]{2,1,0:T(4,128)S(1)} copy(s32[512,4,8]{0,2,1:T(8,128)} %param.8) | data formatting | bytes 131072 | tf_op args[2]
  2.0 1.8 %reshape.32 = s32[4,1,4096]{2,1,0:T(1,128)} reshape(s32[512,4,8]{2,1,0:T(4,128)S(1)} %copy.21) | data formatting | bytes 131072
  3.7 4.2 %all-to-all-start = ((s32[4,1,4096]{2,1,0:T(1,128)}), s32[4,1,4096]{2,1,0:T(1,128)S(1)}, u32[]{:S(2)}, u32[]{:S(2)}) async-start(s32[4,1,4096]{2,1,0:T(1,128)} %reshape.32), calls=%async_computation | async-start | bytes 131072 | tf_op jit(solution)/shard_map/all_to_all | solution.py:22
  8.0 0.1 copy.23
  8.1 0.3 divide_convert_fusion
  8.4 0.4 copy.27
  8.8 3.3 %all-to-all-done = s32[4,1,4096]{2,1,0:T(1,128)S(1)} async-done(((s32[4,1,4096]{2,1,0:T(1,128)}), s32[4,1,4096]{2,1,0:T(1,128)S(1)}, u32[]{:S(2)}, u32[]{:S(2)}) %all-to-all-start) | async-done | bytes 65568 | tf_op jit(solution)/shard_map/all_to_all | solution.py:22
  12.1 0.5 broadcast.11
  12.6 0.8 %reduce.1 = s32[4,4096]{1,0:T(4,128)S(1)} reduce(s32[4,1,4096]{2,1,0:T(1,128)S(1)} %all-to-all-done, s32[]{:T(128)} %broadcast.11), dimensions={1}, to_apply=%all_to_all.15.reduce_sub_computation | reduce | bytes 131076 | tf_op jit(solution)/shard_map/all_to_all | solution.py:22
  13.4 1.3 %reshape.33 = s32[512,4,8]{2,1,0:T(4,128)S(1)} reshape(s32[4,4096]{1,0:T(4,128)S(1)} %reduce.1) | data formatting | bytes 131072
  14.7 0.3 copy.22
  15.0 0.4 convert_reduce_fusion
  15.4 0.2 fusion
  15.7 6.3 %all_to_all.22 = bf16[4,16,256]{2,1,0:T(8,128)(2,1)S(1)} all-to-all(bf16[4,16,256]{2,1,0:T(8,128)(2,1)S(1)} %fusion), channel_id=1, replica_groups=mesh['grp'=8,'lane'=4] {'lane'}, dimensions={0} | all-to-all | bytes 65536 | tf_op jit(solution)/shard_map/all_to_all | solution.py:32
  22.0 0.6 reshape.29
  22.6 6.3 %all-to-all-start.2 = ((bf16[8,2,256]{2,1,0:T(2,128)(2,1)}), bf16[8,2,256]{2,1,0:T(2,128)(2,1)S(1)}, u32[]{:S(2)}, u32[]{:S(2)}) async-start(bf16[8,2,256]{2,1,0:T(2,128)(2,1)} %reshape.29), calls=%async_computation.2 | async-start | bytes 16384 | tf_op jit(solution)/shard_map/all_to_all | solution.py:35
  28.9 0.1 copy.20
  29.1 6.4 %all-to-all-done.2 = bf16[8,2,256]{2,1,0:T(2,128)(2,1)S(1)} async-done(((bf16[8,2,256]{2,1,0:T(2,128)(2,1)}), bf16[8,2,256]{2,1,0:T(2,128)(2,1)S(1)}, u32[]{:S(2)}, u32[]{:S(2)}) %all-to-all-start.2) | async-done | bytes 8224 | tf_op jit(solution)/shard_map/all_to_all | solution.py:35
  35.4 0.4 multiply_reduce_fusion
  35.8 0.6 multiply_reduce_fusion.1
  37.1 38.2 %psum.7 = f32[]{:T(128)} all-reduce(f32[]{:T(128)S(6)} %mul.30), channel_id=1, replica_groups=mesh['grp'=8,'lane'=4] {'grp','lane'}, use_global_device_ids=true, to_apply=%region_4.0 | all-reduce | flops 1 | bytes 8 | tf_op jit(solution)/shard_map/psum | solution.py:44
  76.0 0.6 sqrt_add_fusion
  76.7 1.1 %copy-done.1 = f32[4,256,256]{2,1,0:T(8,128)S(1)} copy-done((f32[4,256,256]{2,1,0:T(8,128)S(1)}, f32[4,256,256]{2,1,0:T(8,128)}, u32[]{:S(2)}) %copy-start.1) | copy-done | bytes 1048600
  77.9 1.2 %divide_subtract_fusion = f32[4,256,256]{2,1,0:T(8,128)} fusion(f32[4,256,256]{2,1,0:T(8,128)S(1)} %copy-done.1, f32[4,256,256]{2,1,0:T(8,128)S(1)} %bitcast.12, f32[4,256]{1,0:T(4,128)S(1)} %get-tuple-element.2), kind=kLoop, calls=%fused_computation.3 | loop fusion | flops 524288 | bytes 3149824 | tf_op jit(solution)/shard_map/sub | solution.py:49
  (17 shorter events, 0.2 us)
Async XLA Ops:
  0.6 7.4 %copy-start.2 = (s32[128,16]{0,1:T(8,128)S(1)}, s32[128,16]{0,1:T(8,128)}, u32[]{:S(2)}) copy-start(s32[128,16]{0,1:T(8,128)} %param.7) | copy-start | bytes 24580
  0.6 7.5 %copy-start = (bf16[128,16,256]{2,1,0:T(8,128)(2,1)S(1)}, bf16[128,16,256]{2,1,0:T(8,128)(2,1)}, u32[]{:S(2)}) copy-start(bf16[128,16,256]{2,1,0:T(8,128)(2,1)} %param.6) | copy-start | bytes 3145732
  3.7 8.4 %all-to-all-start = ((s32[4,1,4096]{2,1,0:T(1,128)}), s32[4,1,4096]{2,1,0:T(1,128)S(1)}, u32[]{:S(2)}, u32[]{:S(2)}) async-start(s32[4,1,4096]{2,1,0:T(1,128)} %reshape.32), calls=%async_computation | async-start | bytes 131072 | tf_op jit(solution)/shard_map/all_to_all | solution.py:22
  15.0 13.9 %copy-start.4 = (s32[1,1,8,2]{2,3,1,0:T(2,128)S(1)}, s32[1,1,8,2]{2,3,1,0:T(2,128)}, u32[]{:S(2)}) copy-start(s32[1,1,8,2]{2,3,1,0:T(2,128)} %param.9) | copy-start | bytes 196
  15.4 60.6 %copy-start.3 = (f32[4,256]{1,0:T(4,128)S(1)}, f32[4,256]{1,0:T(4,128)}, u32[]{:S(2)}) copy-start(f32[4,256]{1,0:T(4,128)} %param.11) | copy-start | bytes 12292
  22.6 12.9 %all-to-all-start.2 = ((bf16[8,2,256]{2,1,0:T(2,128)(2,1)}), bf16[8,2,256]{2,1,0:T(2,128)(2,1)S(1)}, u32[]{:S(2)}, u32[]{:S(2)}) async-start(bf16[8,2,256]{2,1,0:T(2,128)(2,1)} %reshape.29), calls=%async_computation.2 | async-start | bytes 16384 | tf_op jit(solution)/shard_map/all_to_all | solution.py:35
  76.6 1.2 %copy-start.1 = (f32[4,256,256]{2,1,0:T(8,128)S(1)}, f32[4,256,256]{2,1,0:T(8,128)}, u32[]{:S(2)}) copy-start(f32[4,256,256]{2,1,0:T(8,128)} %param.10) | copy-start | bytes 3145732
where the time goes:
time: 79.6 us; the launch traced here: 79 us
  blocking collectives  44.5 us (56%)
  starting transfers between devices  10.6 us (13%)
  waiting for transfers between devices  9.65 us (12%)
  local copies, waits for them, and re-layouts  7.56 us (9%)
  other arithmetic  4.03 us (5%)
  between operations  2.13 us (3%)
    psum x1, blocking collectives, per_device(): norm_total = lax.psum(embed_width * jnp.sum(square_mean), ('grp', 'lane'))  38.2 us
    all_to_all x1, waiting for transfers between devices, per_device(): lax.all_to_all(outgoing, 'grp', split_axis=0, concat_axis=0, tiled=True)  6.35 us
    all_to_all x1, starting transfers between devices, per_device(): lax.all_to_all(outgoing, 'grp', split_axis=0, concat_axis=0, tiled=True)  6.33 us
    all_to_all x1, blocking collectives, per_device(): lax.all_to_all(partial_here, 'lane', split_axis=0, concat_axis=0, tiled=T...  6.3 us
    unnamed x14, local copies, waits for them, and re-layouts  5.6 us
    all_to_all x1, starting transfers between devices, per_device(): lax.all_to_all(lookup_slot, 'lane', split_axis=0, concat_axis=1, tiled=True)  4.24 us
    all_to_all x1, waiting for transfers between devices, per_device(): lax.all_to_all(lookup_slot, 'lane', split_axis=0, concat_axis=1, tiled=True)  3.3 us
  transfers between devices with their start and end apart: 2, of which 2 were waited for; matrix products, arithmetic and copies ran while one was open for 1% of the time, Pallas kernels for 0%

commit v1 on v0

--- a/solution.py
+++ b/solution.py
@@ -19,7 +19,12 @@
     scaled = (grad_pooled.astype(jnp.float32) / bag_len.astype(jnp.float32)[:, :, None]).astype(
         jnp.bfloat16
     )
-    own_slots = lax.all_to_all(lookup_slot, "lane", split_axis=0, concat_axis=1, tiled=True)
+    own_slots = jnp.concatenate(
+        lax.all_to_all(
+            jnp.stack(jnp.split(lookup_slot, lax.axis_size("lane"), axis=0)), "lane", 0, 0
+        ),
+        axis=1,
+    )
     slot_marks = jnp.transpose(
         own_slots.reshape(batch_rows, lane_count, tables_here, bag_depth), (1, 0, 2, 3)
     )

time: 79.6 us -> 74.5 us (0.936)
  local copies, waits for them, and re-layouts: 7.56 us -> 2.63 us
  waiting for transfers between devices: 9.65 us -> 7.73 us
  other arithmetic: 4.03 us -> 5.74 us
    unnamed x14 -> x7, local copies, waits for them, and re-layouts: 5.6 us -> 0.68 us
    all_to_all x1, waiting for transfers between devices: 3.3 us -> 1.38 us  [per_device(): lax.all_to_all(jnp.stack(jnp.split(lookup_slot, lax.axis_size('lane'), ax...]
    convert_element_type x1, other arithmetic: 0.34 us -> 1.57 us  [per_device(): (grad_pooled.astype(jnp.float32) / bag_len.astype(jnp.float32)[:, :, None...]
    all_to_all x1 -> x0, other arithmetic: 0.81 us -> none  [per_device(): lax.all_to_all(lookup_slot, 'lane', split_axis=0, concat_axis=1, tiled=True)]
    all_to_all x2 -> x0, local copies, waits for them, and re-layouts: 0.8 us -> none  [per_device(): lax.all_to_all(lookup_slot, 'lane', split_axis=0, concat_axis=1, tiled=True)]
  transfers between devices with their start and end apart: 2 -> 2, of which waited for: 2 -> 2; matrix products, arithmetic and copies ran while one was open for 1% -> 4% of each run, Pallas kernels for 0% -> 0%
where the time goes in v1:
time: 74.5 us; the launch traced here: 73.9 us
  blocking collectives  44.5 us (60%)
  starting transfers between devices  10.6 us (14%)
  waiting for transfers between devices  7.73 us (10%)
  other arithmetic  5.74 us (8%)
  local copies, waits for them, and re-layouts  2.63 us (4%)
  between operations  2.1 us (3%)
    psum x1, blocking collectives, per_device(): norm_total = lax.psum(embed_width * jnp.sum(square_mean), ('grp', 'lane'))  38.2 us
    all_to_all x1, waiting for transfers between devices, per_device(): lax.all_to_all(outgoing, 'grp', split_axis=0, concat_axis=0, tiled=True)  6.35 us
    all_to_all x1, starting transfers between devices, per_device(): lax.all_to_all(outgoing, 'grp', split_axis=0, concat_axis=0, tiled=True)  6.33 us
    all_to_all x1, blocking collectives, per_device(): lax.all_to_all(partial_here, 'lane', split_axis=0, concat_axis=0, tiled=T...  6.3 us
    all_to_all x1, starting transfers between devices, per_device(): lax.all_to_all(jnp.stack(jnp.split(lookup_slot, lax.axis_size('lane'), ax...  4.24 us
    convert_element_type x1, other arithmetic, per_device(): (grad_pooled.astype(jnp.float32) / bag_len.astype(jnp.float32)[:, :, None...  1.57 us
  transfers between devices with their start and end apart: 2, of which 2 were waited for; matrix products, arithmetic and copies ran while one was open for 4% of the time, Pallas kernels for 0%

profile of v1, /device:TPU:0, one launch (start us, length us, event | category | flops | bytes accessed | tf_op | source)
XLA Modules:
  0.0 73.9 jit_solution(8555533979986851866)
XLA Ops:
  0.6 0.8 %slice_bitcast_fusion.3 = (s32[1,128,4,8]{1,3,2,0:T(8,128)S(1)}, s32[1,128,4,8]{1,3,2,0:T(8,128)S(1)}, s32[1,128,4,8]{1,3,2,0:T(8,128)S(1)}, s32[1,128,4,8]{1,3,2,0:T(8,128)S(1)}) fusion(s32[512,4,8]{0,2,1:T(8,128)} %param.8), kind=kLoop, calls=%fused_computation.16 | loop fusion | bytes 131072 | tf_op jit(solution)/shard_map/stack | solution.py:24
  1.4 0.6 pad_add_fusion
  2.0 4.2 %all-to-all-start = ((s32[4,128,4,8]{1,3,2,0:T(8,128)}), s32[4,128,4,8]{1,3,2,0:T(8,128)S(1)}, u32[]{:S(2)}, u32[]{:S(2)}) async-start(s32[4,128,4,8]{1,3,2,0:T(8,128)} %pad_add_fusion), calls=%async_computation | async-start | bytes 131072 | tf_op jit(solution)/shard_map/all_to_all | solution.py:23
  6.3 0.7 convert_element_type.24
  7.0 0.1 copy.17
  7.1 1.6 %divide_convert_fusion = bf16[128,16,256]{2,1,0:T(8,128)(2,1)S(1)} fusion(bf16[128,16,256]{2,1,0:T(8,128)(2,1)} %param.6, f32[128,16]{1,0:T(8,128)S(1)} %copy.17), kind=kLoop, calls=%fused_computation | loop fusion | flops 1572864 | bytes 2105344 | tf_op jit(solution)/shard_map/convert_element_type | solution.py:19
  8.7 0.4 copy.21
  9.0 0.0 copy-start.2
  9.0 1.4 %all-to-all-done = s32[4,128,4,8]{1,3,2,0:T(8,128)S(1)} async-done(((s32[4,128,4,8]{1,3,2,0:T(8,128)}), s32[4,128,4,8]{1,3,2,0:T(8,128)S(1)}, u32[]{:S(2)}, u32[]{:S(2)}) %all-to-all-start) | async-done | bytes 65568 | tf_op jit(solution)/shard_map/all_to_all | solution.py:23
  10.4 0.4 convert_reduce_fusion
  10.8 0.2 fusion
  11.0 6.3 %all_to_all.15 = bf16[4,16,256]{2,1,0:T(8,128)(2,1)S(1)} all-to-all(bf16[4,16,256]{2,1,0:T(8,128)(2,1)S(1)} %fusion), channel_id=1, replica_groups=mesh['grp'=8,'lane'=4] {'lane'}, dimensions={0} | all-to-all | bytes 65536 | tf_op jit(solution)/shard_map/all_to_all | solution.py:37
  17.3 0.6 reshape.27
  18.0 6.3 %all-to-all-start.2 = ((bf16[8,2,256]{2,1,0:T(2,128)(2,1)}), bf16[8,2,256]{2,1,0:T(2,128)(2,1)S(1)}, u32[]{:S(2)}, u32[]{:S(2)}) async-start(bf16[8,2,256]{2,1,0:T(2,128)(2,1)} %reshape.27), calls=%async_computation.2 | async-start | bytes 16384 | tf_op jit(solution)/shard_map/all_to_all | solution.py:40
  24.3 0.1 copy.16
  24.4 0.1 eq.29
  24.5 6.4 %all-to-all-done.2 = bf16[8,2,256]{2,1,0:T(2,128)(2,1)S(1)} async-done(((bf16[8,2,256]{2,1,0:T(2,128)(2,1)}), bf16[8,2,256]{2,1,0:T(2,128)(2,1)S(1)}, u32[]{:S(2)}, u32[]{:S(2)}) %all-to-all-start.2) | async-done | bytes 8224 | tf_op jit(solution)/shard_map/all_to_all | solution.py:40
  30.8 0.4 multiply_reduce_fusion
  31.2 0.6 multiply_reduce_fusion.1
  32.5 38.2 %psum.7 = f32[]{:T(128)} all-reduce(f32[]{:T(128)S(6)} %mul.30), channel_id=1, replica_groups=mesh['grp'=8,'lane'=4] {'grp','lane'}, use_global_device_ids=true, to_apply=%region_4.0 | all-reduce | flops 1 | bytes 8 | tf_op jit(solution)/shard_map/psum | solution.py:49
  71.4 0.1 broadcast_multiply_fusion
  71.5 0.6 copy-done.1
  72.1 0.6 sqrt_add_fusion
  72.7 1.2 %divide_subtract_fusion = f32[4,256,256]{2,1,0:T(8,128)} fusion(f32[4,256,256]{2,1,0:T(8,128)S(1)} %copy-done, f32[4,256,256]{2,1,0:T(8,128)S(1)} %bitcast.19, f32[4,256]{1,0:T(4,128)S(1)} %get-tuple-element.2), kind=kLoop, calls=%fused_computation.3 | loop fusion | flops 524288 | bytes 3149824 | tf_op jit(solution)/shard_map/sub | solution.py:54
  (9 shorter events, 0.1 us)
Async XLA Ops:
  2.0 8.4 %all-to-all-start = ((s32[4,128,4,8]{1,3,2,0:T(8,128)}), s32[4,128,4,8]{1,3,2,0:T(8,128)S(1)}, u32[]{:S(2)}, u32[]{:S(2)}) async-start(s32[4,128,4,8]{1,3,2,0:T(8,128)} %pad_add_fusion), calls=%async_computation | async-start | bytes 131072 | tf_op jit(solution)/shard_map/all_to_all | solution.py:23
  9.0 15.3 %copy-start.2 = (s32[1,1,8,2]{2,3,1,0:T(2,128)S(1)}, s32[1,1,8,2]{2,3,1,0:T(2,128)}, u32[]{:S(2)}) copy-start(s32[1,1,8,2]{2,3,1,0:T(2,128)} %param.9) | copy-start | bytes 196
  18.0 12.9 %all-to-all-start.2 = ((bf16[8,2,256]{2,1,0:T(2,128)(2,1)}), bf16[8,2,256]{2,1,0:T(2,128)(2,1)S(1)}, u32[]{:S(2)}, u32[]{:S(2)}) async-start(bf16[8,2,256]{2,1,0:T(2,128)(2,1)} %reshape.27), calls=%async_computation.2 | async-start | bytes 16384 | tf_op jit(solution)/shard_map/all_to_all | solution.py:40
  71.4 0.7 copy-start.1
  71.4 1.3 %copy-start = (f32[4,256,256]{2,1,0:T(8,128)S(1)}, f32[4,256,256]{2,1,0:T(8,128)}, u32[]{:S(2)}) copy-start(f32[4,256,256]{2,1,0:T(8,128)} %param.10) | copy-start | bytes 3145732
